TPU v7x, 32 devices: a whole 2x2x4 slice. The times are simulated.
32 devices in a mesh: seq: 16 (over z, y, core), head: 2 (over x).
Axes of the slice: x: 2, y: 2, z: 4, core: 2. Of those that a mesh axis runs over, the one named last changes fastest.
Arguments:
- queries: bfloat16 [2048, 2048], P('seq', 'head'), may hold values from -190 to 190
- key_vectors: bfloat16 [2048, 256], P('seq', 'head'), may hold values from -6.1 to 6.1
- value_vectors: bfloat16 [2048, 256], P('seq', 'head'), may hold values from -54 to 54
- log_gate: float32 [16, 2048], P('head', 'seq'), may hold values from -1 to 0, as said below
- query_map: float32 [16, 128, 128], P('head'), may hold values from -0.5 to 0.5
- key_map: float32 [16, 128, 128], P('head'), may hold values from -0.5 to 0.5
- level_weight: float32 [16, 12], P('head'), may hold values from 0.25 to 2
- norm_gain: float32 [2048], P('head'), may hold values from 0.5 to 1.5
Outputs:
- grad_query_map: float32 [16, 128, 128], P('head')
- grad_key_map: float32 [16, 128, 128], P('head')
- grad_level_weight: float32 [16, 12], P('head')
- grad_norm_gain: float32 [2048], P('head')
Inputs may be any that keep to these rules, and one draw needn't show every extreme that they name: `log_gate`: every entry is negative.
All inputs are finite; a program needn't handle non-finite values.
Results may differ from a plain program's by a relative error of at most 0.0015.
Values may be sent and summed in bfloat16 or wider, within the bound.
No kernel may reach another device: no remote copies, remote signals or barrier semaphores. Data moves between devices by JAX's collectives and lax.ppermute only.
A program may use at most 128 MiB of HBM per device.

v0:
```python
import jax
import jax.numpy as jnp
from jax import lax
from jax.sharding import PartitionSpec as P

HIGHEST = lax.Precision.HIGHEST
NEGATIVE = -1e30
EPSILON = 1e-05


def carried_in(value, axis, join, neutral):
    count, mine = (lax.axis_size(axis), lax.axis_index(axis))
    pieces = lax.all_gather(value, axis)
    subtotal = jnp.full_like(value, 0) + jnp.asarray(neutral, value.dtype)

    def hop(position, subtotal):
        longer = join(subtotal, pieces[position])
        return jnp.where(position < mine, longer, subtotal)

    return lax.fori_loop(0, count - 1, hop, subtotal)


def bit_length(numbers, bit_count):
    digits = jnp.zeros_like(numbers)
    for bit_power in range(bit_count):
        digits = digits + (numbers >= 1 << bit_power).astype(jnp.int32)
    return digits


def teacher_target(query_rows, key_rows, value_rows, first_row):
    span_rows, head_count, head_dim = query_rows.shape
    score_scale = head_dim ** (-0.5)
    positions = first_row + lax.iota(jnp.int32, span_rows)
    row_peak = jnp.full((head_count, span_rows), NEGATIVE, jnp.float32)
    key_piece = lax.all_gather(key_rows, "seq", axis=0, tiled=True)
    value_piece = lax.all_gather(value_rows, "seq", axis=0, tiled=True)
    scores = (
        jnp.einsum("rgd,kd->grk", query_rows, key_piece, preferred_element_type=jnp.float32)
        * score_scale
    )
    key_pos = lax.iota(jnp.int32, key_piece.shape[0])
    scores = jnp.where(key_pos[None, None, :] <= positions[None, :, None], scores, NEGATIVE)
    new_peak = jnp.maximum(row_peak, jnp.max(scores, axis=2))
    weights = jnp.exp(scores - new_peak[..., None])
    update = jnp.einsum(
        "grk,kd->grd", weights.astype(jnp.bfloat16), value_piece, preferred_element_type=jnp.float32
    )
    row_total = jnp.sum(weights, axis=2)
    return update / row_total[..., None]


def fenwick_gathered(raw_state, ending, before, span_id, span_bits):
    initial = jnp.zeros((span_bits,) + raw_state.shape, jnp.float32)
    piece_states = lax.all_gather(raw_state[None], "seq", axis=0, tiled=True)
    piece_ends = lax.all_gather(ending[None], "seq", axis=0, tiled=True)
    piece_count = piece_states.shape[0]
    source_id = lax.iota(jnp.int32, piece_count)
    level_id = bit_length(jnp.bitwise_xor(source_id, span_id), span_bits)
    earlier = source_id < span_id
    exponent = jnp.where(earlier[:, None], before[None, :] - piece_ends, NEGATIVE)
    link_decay = jnp.exp(exponent)
    level_pick = (level_id[:, None] == (1 + lax.iota(jnp.int32, span_bits))[None, :]).astype(
        jnp.float32
    )
    coupling = level_pick[:, :, None] * link_decay[:, None, :]
    return initial + jnp.einsum("njg,ngab->jgab", coupling, piece_states, precision=HIGHEST)


def on_device(
    queries, key_vectors, value_vectors, log_gate, query_map, key_map, level_weight, norm_gain
):
    span_rows, head_dim = key_vectors.shape
    head_count = queries.shape[1] // head_dim
    seq_count = lax.axis_size("seq")
    span_id = lax.axis_index("seq")
    span_bits = seq_count.bit_length() - 1
    low_bits = span_rows.bit_length() - 1
    total_tokens = span_rows * seq_count
    norm_width = head_count * head_dim * lax.axis_size("head")
    query_rows = queries.reshape(span_rows, head_count, head_dim)
    target = teacher_target(query_rows, key_vectors, value_vectors, span_id * span_rows)
    local_cum = jnp.cumsum(log_gate, axis=1)
    before = carried_in(
        local_cum[:, -1],
        "seq",
        lambda earlier, later_term: earlier + later_term,
        jnp.zeros((head_count,), jnp.float32),
    )
    cumulative = before[:, None] + local_cum
    ending = cumulative[:, -1]
    query_float = query_rows.astype(jnp.float32)
    keys_float = key_vectors.astype(jnp.float32)
    values_float = value_vectors.astype(jnp.float32)
    query_proj = jnp.einsum("rgd,gde->gre", query_float, query_map, precision=HIGHEST)
    key_proj = jnp.einsum("rd,gde->gre", keys_float, key_map, precision=HIGHEST)
    position = lax.iota(jnp.int32, span_rows)
    causal = position[None, :] <= position[:, None]
    local_level = bit_length(jnp.bitwise_xor(position[:, None], position[None, :]), low_bits)
    decay_in = jnp.exp(
        jnp.where(causal[None], cumulative[:, :, None] - cumulative[:, None, :], NEGATIVE)
    )
    level_mask = jnp.zeros_like(decay_in)
    for level_id in range(low_bits + 1):
        level_mask = (
            level_mask
            + level_weight[:, level_id][:, None, None]
            * (local_level == level_id).astype(jnp.float32)[None]
        )
    mix_weight = decay_in * level_mask
    scores = jnp.einsum("gre,gse->grs", query_proj, key_proj, precision=HIGHEST)
    local_part = jnp.einsum("grs,sd->grd", scores * mix_weight, values_float, precision=HIGHEST)
    raw_state = jnp.einsum(
        "gsa,sb->gab",
        jnp.exp(ending[:, None] - cumulative)[:, :, None] * keys_float[None],
        values_float,
        precision=HIGHEST,
    )
    level_states = fenwick_gathered(raw_state, ending, before, span_id, span_bits)
    cross_weight = level_weight[:, low_bits + 1 :]
    combined = jnp.einsum("gj,jgab->gab", cross_weight, level_states, precision=HIGHEST)
    key_state = jnp.einsum("gba,gbf->gaf", key_map, combined, precision=HIGHEST)
    entry_decay = jnp.exp(cumulative - before[:, None])
    far_part = entry_decay[:, :, None] * jnp.einsum(
        "gre,gef->grf", query_proj, key_state, precision=HIGHEST
    )
    student_raw = local_part + far_part
    square_sum = lax.psum(jnp.sum(student_raw * student_raw, axis=(0, 2)), "head")
    inverse = lax.rsqrt(square_sum / norm_width + EPSILON)
    gain_rows = norm_gain.reshape(head_count, 1, head_dim)
    normed = student_raw * inverse[None, :, None]
    mismatch = (normed * gain_rows - target) / total_tokens
    grad_gain = jnp.sum(mismatch * normed, axis=1).reshape(-1)
    scaled_cot = mismatch * gain_rows
    inner_sum = lax.psum(jnp.sum(scaled_cot * student_raw, axis=(0, 2)), "head")
    residual = (
        inverse[None, :, None] * scaled_cot
        - student_raw * (inverse * inverse * inverse * inner_sum / norm_width)[None, :, None]
    )
    d_mix = jnp.einsum("grd,sd->grs", residual, values_float, precision=HIGHEST)
    d_scores = d_mix * mix_weight
    through = d_mix * scores * decay_in
    local_grads = [
        jnp.sum(through * (local_level == level_id).astype(jnp.float32)[None], axis=(1, 2))
        for level_id in range(low_bits + 1)
    ]
    d_state = jnp.einsum(
        "gre,grf->gef", entry_decay[:, :, None] * query_proj, residual, precision=HIGHEST
    )
    d_combined = jnp.einsum("gba,gaf->gbf", key_map, d_state, precision=HIGHEST)
    d_query = jnp.einsum("grs,gse->gre", d_scores, key_proj, precision=HIGHEST) + entry_decay[
        :, :, None
    ] * jnp.einsum("grf,gef->gre", residual, key_state, precision=HIGHEST)
    d_key = jnp.einsum("grs,gre->gse", d_scores, query_proj, precision=HIGHEST)
    grad_query = jnp.einsum("rgb,gre->gbe", query_float, d_query, precision=HIGHEST)
    grad_key = jnp.einsum("gbf,gaf->gba", combined, d_state, precision=HIGHEST) + jnp.einsum(
        "rb,gre->gbe", keys_float, d_key, precision=HIGHEST
    )
    cross_grads = jnp.einsum("jgab,gab->gj", level_states, d_combined, precision=HIGHEST)
    grad_levels = jnp.concatenate([jnp.stack(local_grads, axis=1), cross_grads], axis=1)
    return lax.psum((grad_query, grad_key, grad_levels, grad_gain), "seq")


def solution(mesh):
    placed = (
        P("seq", "head"),
        P("seq", "head"),
        P("seq", "head"),
        P("head", "seq"),
        P("head", None, None),
        P("head", None, None),
        P("head", None),
        P("head"),
    )
    return jax.shard_map(
        on_device,
        mesh=mesh,
        in_specs=placed,
        out_specs=(P("head", None, None), P("head", None, None), P("head", None), P("head")),
        check_vma=False,
    )
```

profile of v0, /device:TPU:0, one launch (start us, length us, event | category | flops | bytes accessed | tf_op | source)
XLA Modules:
  0.0 298.1 jit_solution(158469904230548614)
XLA Ops:
  7.3 1.0 reduce_window_sum.11
  8.4 1.2 dynamic-slice
  10.6 34.9 %all-reduce = f32[128]{0:T(128)S(1)} all-reduce(f32[128]{0:T(128)S(1)} %dynamic-update-slice), channel_id=2, replica_groups=mesh['seq'=16,'head'=2] {'seq'}, use_global_device_ids=true, to_apply=%add | all-reduce | flops 128 | bytes 1024
  47.4 1.9 fusion.25
  50.4 30.4 %all-reduce.1 = f32[128]{0:T(128)S(1)} all-reduce(f32[128]{0:T(128)S(1)} %dynamic-update-slice.1), channel_id=4, replica_groups=mesh['seq'=16,'head'=2] {'seq'}, use_global_device_ids=true, to_apply=%add.1 | all-reduce | flops 128 | bytes 1024
  81.0 1.3 slice_reduce_fusion.8
  84.2 22.4 %all_gather.18 = bf16[2048,128]{1,0:T(8,128)(2,1)S(1)} all-gather(bf16[128,128]{1,0:T(8,128)(2,1)} %param.11), channel_id=1, replica_groups=mesh['seq'=16,'head'=2] {'seq'}, dimensions={0}, use_global_device_ids=true | all-gather | bytes 557056 | tf_op jit(solution)/shard_map/all_gather | solution.py:35
  106.7 2.3 fusion.4
  109.7 23.8 %all_gather.19 = bf16[2048,128]{1,0:T(8,128)(2,1)} all-gather(bf16[128,128]{1,0:T(8,128)(2,1)S(1)} %copy-done.14), channel_id=1, replica_groups=mesh['seq'=16,'head'=2] {'seq'}, dimensions={0}, use_global_device_ids=true | all-gather | bytes 557056 | tf_op jit(solution)/shard_map/all_gather | solution.py:36
  135.4 1.6 fusion.27
  137.1 2.3 fusion.2
  139.4 12.5 %fusion = f32[8,128,128,4]{2,3,1,0:T(4,128)S(1)} fusion(f32[16,8,128,128]{3,2,1,0:T(8,128)} %bitcast.126, f32[16,8]{0,1:T(8,128)} %select_exponential_fusion.1, f32[16,4]{0,1:T(4,128)} %compare_convert_fusion.8), kind=kOutput, calls=%fused_computation.3 | convolution fusion | flops 100663808 | bytes 10486528 | tf_op jit(solution)/shard_map/njg,ngab->jgab/dot_general | solution.py:66
  151.9 3.8 %fusion.10 = f32[8,1,128,128]{3,1,2,0:T(1,128)S(1)} fusion(f32[8,4,1,1]{1,2,3,0:T(1,128)S(1)} %bitcast.129, f32[8,128,128,4]{2,3,1,0:T(4,128)S(1)} %fusion), kind=kOutput, calls=%fused_computation.13 | convolution fusion | flops 6291456 | bytes 2621568 | tf_op jit(solution)/shard_map/gj,jgab->gab/dot_general | solution.py:120
  156.6 1.0 fusion.69
  158.4 2.5 multiply_reduce_fusion.10
  160.9 5.5 %psum.42 = f32[128]{0:T(128)} all-reduce(f32[128]{0:T(128)} %get-tuple-element.153), channel_id=1, replica_groups=mesh['seq'=16,'head'=2] {'head'}, use_global_device_ids=true, to_apply=%region_4.5 | all-reduce | flops 128 | bytes 1024 | tf_op jit(solution)/shard_map/psum | solution.py:127
  167.1 7.1 %multiply_reduce_fusion = (f32[8,128]{1,0:T(8,128)}, f32[128]{0:T(128)}, f32[8,128,128]{2,1,0:T(8,128)}) fusion(f32[8,128,128]{2,1,0:T(8,128)} %get-tuple-element.154, f32[128]{0:T(128)S(1)} %add_rsqrt_fusion, f32[8,128]{1,0:T(8,128)} %get-tuple-element.167, f32[8,128]{1,0:T(8,128)} %fusion.2, bf16[2048,128]{1,0:T(8,128)(2,1)} %all_gather.19, ...), kind=kOutput, calls=%fused_computation.29 | convolution fusion | flops 546569088 | bytes 10245120 | tf_op jit(solution)/shard_map/grk,kd->grd/dot_general | solution.py:45
  174.2 5.8 %psum.43 = f32[128]{0:T(128)} all-reduce(f32[128]{0:T(128)} %get-tuple-element.120), channel_id=1, replica_groups=mesh['seq'=16,'head'=2] {'head'}, use_global_device_ids=true, to_apply=%region_8.9 | all-reduce | flops 128 | bytes 1024 | tf_op jit(solution)/shard_map/psum | solution.py:134
  180.8 1.3 multiply_subtract_fusion
  182.2 2.7 multiply_reduce_fusion.1
  184.9 2.9 fusion.38
  187.8 2.4 fusion.36
  190.3 1.2 fusion.23
  192.6 1.4 convolution_bitcast_fusion.1
  194.0 2.0 convolution_add_fusion
  196.0 2.1 convolution_bitcast_fusion.2
  198.1 1.3 copy.155
  200.1 9.6 %fusion.8 = f32[8,1,4,1]{2,1,3,0:T(1,128)S(1)} fusion(f32[8,128,128,1]{2,3,1,0:T(1,128)} %copy.155, f32[8,128,128,4]{2,3,1,0:T(4,128)S(1)} %fusion), kind=kOutput, calls=%fused_computation.11 | convolution fusion | flops 6291456 | bytes 2621568 | tf_op jit(solution)/shard_map/jgab,gab->gj/dot_general | solution.py:158
  209.8 30.6 %all-reduce.2 = (f32[8,12]{1,0:T(8,128)}, f32[1024]{0:T(1024)}) all-reduce(f32[8,12]{1,0:T(8,128)S(1)} %concatenate.3, f32[1024]{0:T(1024)S(1)} %bitcast.131), channel_id=1, replica_groups=mesh['seq'=16,'head'=2] {'seq'}, use_global_device_ids=true, to_apply=%region_19.20 | all-reduce | flops 1120 | bytes 8960 | tf_op jit(solution)/shard_map/psum | solution.py:160
  240.4 47.0 %all-reduce.6.cloned.1.call-done = (f32[8,128,128]{1,2,0:T(8,128)}, f32[8,128,128]{2,1,0:T(8,128)}) async-done(((f32[8,128,128]{1,2,0:T(8,128)}, f32[8,128,128]{2,1,0:T(8,128)}), (f32[8,128,128]{1,2,0:T(8,128)}, f32[8,128,128]{2,1,0:T(8,128)})) %all-reduce.6.cloned.1.call-update) | async-done | bytes 1048592 | tf_op jit(solution)/shard_map/psum | solution.py:160
  287.4 2.0 copy.139
  289.4 1.9 copy.186
  (146 shorter events, 12.9 us)
Async XLA Ops:
  7.2 126.4 %copy-start = (f32[8,128,128]{2,1,0:T(8,128)S(1)}, f32[8,128,128]{2,1,0:T(8,128)}, u32[]{:S(2)}) copy-start(f32[8,128,128]{2,1,0:T(8,128)} %param.15) | copy-start | bytes 1572868
  7.2 132.2 %all-gather.5.cloned.1.call-start = ((), (), s32[]{:S(2)}) async-start(), calls=%async_computation | async-start | bytes 8912896 | tf_op jit(solution)/shard_map/all_gather | solution.py:54
  46.2 62.8 %copy-start.25 = (f32[1024]{0:T(1024)S(1)}, f32[1024]{0:T(1024)}, u32[]{:S(2)}) copy-start(f32[1024]{0:T(1024)} %param.17) | copy-start | bytes 12292
  46.2 63.5 %copy-start.14 = (bf16[128,128]{1,0:T(8,128)(2,1)S(1)}, bf16[128,128]{1,0:T(8,128)(2,1)}, u32[]{:S(2)}) copy-start(bf16[128,128]{1,0:T(8,128)(2,1)} %param.12) | copy-start | bytes 98308
  49.4 84.2 %copy-start.12 = (bf16[128,128]{1,0:T(8,128)(2,1)S(1)}, bf16[128,128]{1,0:T(8,128)(2,1)}, u32[]{:S(2)}) copy-start(bf16[128,128]{1,0:T(8,128)(2,1)} %param.11) | copy-start | bytes 98308
  49.4 238.0 %all-reduce.6.cloned.1.call-start = ((), (), s32[]{:S(2)}) async-start(), calls=%async_computation.1 | async-start | bytes 2097152 | tf_op jit(solution)/shard_map/psum | solution.py:160
  82.3 53.0 %copy-start.26 = (f32[8]{0:T(128)}, f32[8]{0:T(128)S(1)}, u32[]{:S(2)}) copy-start(f32[8]{0:T(128)S(1)} %get-tuple-element.129) | copy-start | bytes 100
  82.3 53.0 %copy-start.27 = (f32[8]{0:T(128)}, f32[8]{0:T(128)S(1)}, u32[]{:S(2)}) copy-start(f32[8]{0:T(128)S(1)} %get-tuple-element.130) | copy-start | bytes 100
  82.3 53.0 %copy-start.28 = (f32[8]{0:T(128)}, f32[8]{0:T(128)S(1)}, u32[]{:S(2)}) copy-start(f32[8]{0:T(128)S(1)} %get-tuple-element.131) | copy-start | bytes 100
  82.3 53.0 %copy-start.29 = (f32[8]{0:T(128)}, f32[8]{0:T(128)S(1)}, u32[]{:S(2)}) copy-start(f32[8]{0:T(128)S(1)} %get-tuple-element.132) | copy-start | bytes 100
  82.3 53.0 %copy-start.30 = (f32[8]{0:T(128)}, f32[8]{0:T(128)S(1)}, u32[]{:S(2)}) copy-start(f32[8]{0:T(128)S(1)} %get-tuple-element.133) | copy-start | bytes 100
  82.4 53.0 %copy-start.31 = (f32[8]{0:T(128)}, f32[8]{0:T(128)S(1)}, u32[]{:S(2)}) copy-start(f32[8]{0:T(128)S(1)} %get-tuple-element.134) | copy-start | bytes 100
  82.4 53.0 %copy-start.32 = (f32[8]{0:T(128)}, f32[8]{0:T(128)S(1)}, u32[]{:S(2)}) copy-start(f32[8]{0:T(128)S(1)} %get-tuple-element.135) | copy-start | bytes 100
  82.4 53.0 %copy-start.33 = (f32[8]{0:T(128)}, f32[8]{0:T(128)S(1)}, u32[]{:S(2)}) copy-start(f32[8]{0:T(128)S(1)} %get-tuple-element.136) | copy-start | bytes 100
  82.4 52.9 %copy-start.15 = (f32[128,128]{1,0:T(8,128)}, f32[128,128]{1,0:T(8,128)S(1)}, u32[]{:S(2)}) copy-start(f32[128,128]{1,0:T(8,128)S(1)} %compare_convert_fusion.7) | copy-start | bytes 196612
  82.5 52.8 %copy-start.23 = (pred[128,128]{1,0:T(8,128)(4,1)}, pred[128,128]{1,0:T(8,128)(4,1)S(1)}, u32[]{:S(2)}) copy-start(pred[128,128]{1,0:T(8,128)(4,1)S(1)} %get-tuple-element.159) | copy-start | bytes 49156
  82.6 52.7 %copy-start.16 = (f32[128,128]{1,0:T(8,128)}, f32[128,128]{1,0:T(8,128)S(1)}, u32[]{:S(2)}) copy-start(f32[128,128]{1,0:T(8,128)S(1)} %get-tuple-element.165) | copy-start | bytes 196612
  82.6 52.7 %copy-start.17 = (f32[128,128]{1,0:T(8,128)}, f32[128,128]{1,0:T(8,128)S(1)}, u32[]{:S(2)}) copy-start(f32[128,128]{1,0:T(8,128)S(1)} %get-tuple-element.166) | copy-start | bytes 196612
  82.6 51.5 %copy-start.7 = (bf16[128,1024]{1,0:T(8,128)(2,1)S(1)}, bf16[128,1024]{1,0:T(8,128)(2,1)}, u32[]{:S(2)}) copy-start(bf16[128,1024]{1,0:T(8,128)(2,1)} %param.10) | copy-start | bytes 786436
  82.6 51.5 %copy-start.13 = (f32[8,128,128]{2,1,0:T(8,128)S(1)}, f32[8,128,128]{2,1,0:T(8,128)}, u32[]{:S(2)}) copy-start(f32[8,128,128]{2,1,0:T(8,128)} %param.14) | copy-start | bytes 1572868
  82.7 52.7 %copy-start.18 = (f32[128,128]{1,0:T(8,128)}, f32[128,128]{1,0:T(8,128)S(1)}, u32[]{:S(2)}) copy-start(f32[128,128]{1,0:T(8,128)S(1)} %get-tuple-element.163) | copy-start | bytes 196612
  82.7 52.7 %copy-start.19 = (f32[128,128]{1,0:T(8,128)}, f32[128,128]{1,0:T(8,128)S(1)}, u32[]{:S(2)}) copy-start(f32[128,128]{1,0:T(8,128)S(1)} %get-tuple-element.164) | copy-start | bytes 196612
  82.8 52.6 %copy-start.20 = (f32[128,128]{1,0:T(8,128)}, f32[128,128]{1,0:T(8,128)S(1)}, u32[]{:S(2)}) copy-start(f32[128,128]{1,0:T(8,128)S(1)} %get-tuple-element.161) | copy-start | bytes 196612
  82.8 52.6 %copy-start.21 = (f32[128,128]{1,0:T(8,128)}, f32[128,128]{1,0:T(8,128)S(1)}, u32[]{:S(2)}) copy-start(f32[128,128]{1,0:T(8,128)S(1)} %get-tuple-element.162) | copy-start | bytes 196612
  109.0 28.0 %copy-start.1 = (f32[2048,128,8]{1,0,2:T(8,128)}, f32[2048,128,8]{1,0,2:T(8,128)S(1)}, u32[]{:S(2)}) copy-start(f32[2048,128,8]{1,0,2:T(8,128)S(1)} %get-tuple-element.152) | copy-start | bytes 25165828
  139.4 19.0 %copy-start.11 = (f32[8,128,128]{2,1,0:T(8,128)S(1)}, f32[8,128,128]{2,1,0:T(8,128)}, u32[]{:S(2)}) copy-start(f32[8,128,128]{2,1,0:T(8,128)} %fusion.27) | copy-start | bytes 1572868
  160.9 19.9 %copy-start.22 = (f32[8,128]{1,0:T(8,128)S(1)}, f32[8,128]{1,0:T(8,128)}, u32[]{:S(2)}) copy-start(f32[8,128]{1,0:T(8,128)} %get-tuple-element.167) | copy-start | bytes 12292
  174.2 18.3 %copy-start.8 = (bf16[128,1024]{1,0:T(8,128)(2,1)S(1)}, bf16[128,1024]{1,0:T(8,128)(2,1)}, u32[]{:S(2)}) copy-start(bf16[128,1024]{1,0:T(8,128)(2,1)} %param.10) | copy-start | bytes 786436
  184.9 14.7 %copy-start.37 = (f32[8]{0:T(128)S(1)}, f32[8]{0:T(128)}, u32[]{:S(2)}) copy-start(f32[8]{0:T(128)} %get-tuple-element.124) | copy-start | bytes 100
  184.9 14.8 %copy-start.36 = (f32[8]{0:T(128)S(1)}, f32[8]{0:T(128)}, u32[]{:S(2)}) copy-start(f32[8]{0:T(128)} %get-tuple-element.125) | copy-start | bytes 100
  184.9 14.9 %copy-start.35 = (f32[8]{0:T(128)S(1)}, f32[8]{0:T(128)}, u32[]{:S(2)}) copy-start(f32[8]{0:T(128)} %get-tuple-element.126) | copy-start | bytes 100
  190.3 19.5 %copy-start.24 = (f32[8,128]{1,0:T(8,128)S(1)}, f32[8,128]{1,0:T(8,128)}, u32[]{:S(2)}) copy-start(f32[8,128]{1,0:T(8,128)} %get-tuple-element.119) | copy-start | bytes 12292
  (11 other events, 89.6 us)
Sparse Core Ops, SparseCore 0:
  49.5 77.1 all-gather.4
  196.1 91.1 all-reduce.5
where the time goes:
time: 299 us; the launch traced here: 298 us
  blocking collectives  154 us (52%)
  matrix products  60 us (20%)
  waiting for transfers between devices  47 us (16%)
  between operations  15.3 us (5%)
  local copies, waits for them, and re-layouts  12.9 us (4%)
  other arithmetic  8.97 us (3%)
    unnamed x2, blocking collectives  65.4 us
    psum x1, waiting for transfers between devices, on_device(): return lax.psum((grad_query, grad_key, grad_levels, grad_gain), 'seq')  47 us
    psum x1, blocking collectives, on_device(): return lax.psum((grad_query, grad_key, grad_levels, grad_gain), 'seq')  30.6 us
    all_gather x1, blocking collectives, teacher_target(): value_piece = lax.all_gather(value_rows, 'seq', axis=0, tiled=True)  23.8 us
    all_gather x1, blocking collectives, teacher_target(): key_piece = lax.all_gather(key_rows, 'seq', axis=0, tiled=True)  22.4 us
    dot_general x1, matrix products, fenwick_gathered(): jnp.einsum('njg,ngab->jgab', coupling, piece_states, precision=HIGHEST)  12.5 us
    dot_general x1, matrix products, on_device(): jnp.einsum('jgab,gab->gj', level_states, d_combined, precision=HIGHEST)  9.65 us
    unnamed x89, local copies, waits for them, and re-layouts  7.34 us
  transfers between devices with their start and end apart: 2, of which 1 were waited for; matrix products, arithmetic and copies ran while one was open for 9% of the time, Pallas kernels for 0%

commit v1 on v0

--- a/solution.py
+++ b/solution.py
@@ -2,10 +2,18 @@
 import jax.numpy as jnp
 from jax import lax
 from jax.sharding import PartitionSpec as P
+from jax.lax import all_gather
 
 HIGHEST = lax.Precision.HIGHEST
 NEGATIVE = -1e30
 EPSILON = 1e-05
+
+
+def corner_review(q_in, arr_in):
+    answer = jnp.concatenate([arr_in, q_in], axis=1)
+    reply = all_gather(answer, "seq", axis=0, tiled=True)
+    arr_now = jnp.split(reply, [arr_in.shape[1]], axis=1)
+    return arr_now
 
 
 def carried_in(value, axis, join, neutral):
@@ -32,8 +40,7 @@
     score_scale = head_dim ** (-0.5)
     positions = first_row + lax.iota(jnp.int32, span_rows)
     row_peak = jnp.full((head_count, span_rows), NEGATIVE, jnp.float32)
-    key_piece = lax.all_gather(key_rows, "seq", axis=0, tiled=True)
-    value_piece = lax.all_gather(value_rows, "seq", axis=0, tiled=True)
+    key_piece, value_piece = corner_review(value_rows, arr_in=key_rows)
     scores = (
         jnp.einsum("rgd,kd->grk", query_rows, key_piece, preferred_element_type=jnp.float32)
         * score_scale

time: 299 us -> 286 us (0.957)
  blocking collectives: 154 us -> 107 us
  waiting for transfers between devices: 47 us -> 73.6 us
  local copies, waits for them, and re-layouts: 12.9 us -> 17.3 us
    all_gather x2 -> x0, blocking collectives: 46.2 us -> none  [the longest x1 23.8 us: teacher_target(): value_piece = lax.all_gather(value_rows, 'seq', axis=0, tiled=True)]
    all_gather x1, waiting for transfers between devices: 0.01 us -> 25.1 us  [fenwick_gathered(): piece_states = lax.all_gather(raw_state[None], 'seq', axis=0, tiled=True)]
    unnamed x89 -> x87, local copies, waits for them, and re-layouts: 7.34 us -> 11.7 us
  transfers between devices with their start and end apart: 2 -> 3, of which waited for: 1 -> 2; matrix products, arithmetic and copies ran while one was open for 9% -> 12% of each run, Pallas kernels for 0% -> 0%
where the time goes in v1:
time: 286 us; the launch traced here: 285 us
  blocking collectives  107 us (37%)
  waiting for transfers between devices  73.6 us (26%)
  matrix products  62.5 us (22%)
  local copies, waits for them, and re-layouts  17.3 us (6%)
  between operations  15 us (5%)
  other arithmetic  9.22 us (3%)
    unnamed x2, blocking collectives  65.8 us
    psum x1, waiting for transfers between devices, on_device(): return lax.psum((grad_query, grad_key, grad_levels, grad_gain), 'seq')  48.4 us
    psum x1, blocking collectives, on_device(): return lax.psum((grad_query, grad_key, grad_levels, grad_gain), 'seq')  30.8 us
    all_gather x1, waiting for transfers between devices, fenwick_gathered(): piece_states = lax.all_gather(raw_state[None], 'seq', axis=0, tiled=True)  25.1 us
    dot_general x1, matrix products, fenwick_gathered(): jnp.einsum('njg,ngab->jgab', coupling, piece_states, precision=HIGHEST)  12.4 us
    unnamed x87, local copies, waits for them, and re-layouts  11.7 us
    dot_general x1, matrix products, on_device(): jnp.einsum('jgab,gab->gj', level_states, d_combined, precision=HIGHEST)  9.66 us
    dot_general x1, matrix products, teacher_target(): jnp.einsum('grk,kd->grd', weights.astype(jnp.bfloat16), value_piece, pref...  7.11 us
  transfers between devices with their start and end apart: 3, of which 2 were waited for; matrix products, arithmetic and copies ran while one was open for 12% of the time, Pallas kernels for 0%

profile of v1, /device:TPU:0, one launch (start us, length us, event | category | flops | bytes accessed | tf_op | source)
XLA Modules:
  0.0 285.3 jit_solution(17341588087106676626)
XLA Ops:
  7.2 1.5 pad_maximum_fusion
  10.0 1.2 dynamic-slice
  12.1 35.1 %all-reduce = f32[128]{0:T(128)S(1)} all-reduce(f32[128]{0:T(128)S(1)} %dynamic-update-slice), channel_id=2, replica_groups=mesh['seq'=16,'head'=2] {'seq'}, use_global_device_ids=true, to_apply=%add | all-reduce | flops 128 | bytes 1024
  49.1 2.0 fusion.23
  52.1 30.7 %all-reduce.1 = f32[128]{0:T(128)S(1)} all-reduce(f32[128]{0:T(128)S(1)} %dynamic-update-slice.1), channel_id=4, replica_groups=mesh['seq'=16,'head'=2] {'seq'}, use_global_device_ids=true, to_apply=%add.1 | all-reduce | flops 128 | bytes 1024
  82.9 1.3 slice_reduce_fusion.8
  86.7 1.3 fusion.53
  88.1 1.7 fusion.29
  91.3 2.4 fusion.25
  94.0 2.5 fusion.4
  96.5 3.2 %copy-done.1 = f32[2048,128,8]{1,0,2:T(8,128)} copy-done((f32[2048,128,8]{1,0,2:T(8,128)}, f32[2048,128,8]{1,0,2:T(8,128)S(1)}, u32[]{:S(2)}) %copy-start.1) | copy-done | bytes 8388632
  99.7 1.7 fusion.2
  101.4 25.1 %all-gather.8.cloned.1.call-done = f32[128,128,128]{2,1,0:T(8,128)} async-done(((f32[8,128,128]{2,1,0:T(8,128)}), f32[128,128,128]{2,1,0:T(8,128)}) %all-gather.8.cloned.1.call-update) | async-done | bytes 8388624 | tf_op jit(solution)/shard_map/all_gather | solution.py:61
  126.5 12.4 %fusion = f32[8,128,128,4]{2,3,1,0:T(4,128)S(1)} fusion(f32[16,8,128,128]{3,2,1,0:T(8,128)} %bitcast.126, f32[16,8]{0,1:T(8,128)} %select_exponential_fusion.1, f32[16,4]{0,1:T(4,128)} %compare_convert_fusion.8), kind=kOutput, calls=%fused_computation.3 | convolution fusion | flops 100663808 | bytes 10486528 | tf_op jit(solution)/shard_map/njg,ngab->jgab/dot_general | solution.py:73
  138.9 4.0 %fusion.10 = f32[8,1,128,128]{3,1,2,0:T(1,128)S(1)} fusion(f32[8,4,1,1]{1,2,3,0:T(1,128)S(1)} %bitcast.129, f32[8,128,128,4]{2,3,1,0:T(4,128)S(1)} %fusion), kind=kOutput, calls=%fused_computation.13 | convolution fusion | flops 6291456 | bytes 2621568 | tf_op jit(solution)/shard_map/gj,jgab->gab/dot_general | solution.py:127
  145.6 2.0 multiply_reduce_fusion.10
  147.6 4.9 %psum.42 = f32[128]{0:T(128)S(1)} all-reduce(f32[128]{0:T(128)S(1)} %get-tuple-element.153), channel_id=1, replica_groups=mesh['seq'=16,'head'=2] {'head'}, use_global_device_ids=true, to_apply=%region_4.5 | all-reduce | flops 128 | bytes 1024 | tf_op jit(solution)/shard_map/psum | solution.py:134
  153.1 7.1 %multiply_reduce_fusion = (f32[8,128]{1,0:T(8,128)S(1)}, f32[128]{0:T(128)}, f32[8,128,128]{2,1,0:T(8,128)}) fusion(f32[8,128,128]{2,1,0:T(8,128)} %get-tuple-element.154, f32[128]{0:T(128)S(1)} %add_rsqrt_fusion, f32[8,128]{1,0:T(8,128)S(1)} %broadcast_multiply_fusion, f32[8,128]{1,0:T(8,128)S(1)} %fusion.2, ...), kind=kOutput, calls=%fused_computation.29 | convolution fusion | flops 546569088 | bytes 10245120 | tf_op jit(solution)/shard_map/grk,kd->grd/dot_general | solution.py:52
  160.2 5.8 %psum.43 = f32[128]{0:T(128)} all-reduce(f32[128]{0:T(128)} %get-tuple-element.120), channel_id=1, replica_groups=mesh['seq'=16,'head'=2] {'head'}, use_global_device_ids=true, to_apply=%region_8.9 | all-reduce | flops 128 | bytes 1024 | tf_op jit(solution)/shard_map/psum | solution.py:141
  166.7 1.3 multiply_subtract_fusion
  168.1 2.7 multiply_reduce_fusion.1
  170.8 2.9 %fusion.36 = f32[8,128,128]{2,1,0:T(8,128)S(1)} fusion(f32[8,128,128]{2,1,0:T(8,128)} %copy-done.7, f32[8,128,128]{2,1,0:T(8,128)S(1)} %get-tuple-element.158, f32[128,128]{1,0:T(8,128)S(1)} %get-tuple-element.160, f32[8]{0:T(128)} %copy-done.30, f32[128,128]{1,0:T(8,128)} %copy-done.19, f32[8]{0:T(128)} %copy-done.24, f32[128,128]{1,0:T(8,128)} %copy-done.20, ...), kind=kOutput, calls=%fused_computation.59 | convolution fusion | flops 203816960 | bytes 2117888 | tf_op jit(solution)/shard_map/grs,gse->gre/dot_general | solution.py:157
  173.7 2.4 fusion.34
  178.5 1.4 convolution_bitcast_fusion.1
  179.8 2.0 convolution_add_fusion
  181.9 2.1 convolution_bitcast_fusion.2
  183.9 1.3 copy.155
  185.9 9.7 %fusion.8 = f32[8,1,4,1]{2,1,3,0:T(1,128)S(1)} fusion(f32[8,128,128,1]{2,3,1,0:T(1,128)} %copy.155, f32[8,128,128,4]{2,3,1,0:T(4,128)S(1)} %fusion), kind=kOutput, calls=%fused_computation.11 | convolution fusion | flops 6291456 | bytes 2621568 | tf_op jit(solution)/shard_map/jgab,gab->gj/dot_general | solution.py:165
  195.7 30.8 %all-reduce.2 = (f32[8,12]{1,0:T(8,128)}, f32[1024]{0:T(1024)}) all-reduce(f32[8,12]{1,0:T(8,128)S(1)} %concatenate.7, f32[1024]{0:T(1024)S(1)} %bitcast.132), channel_id=1, replica_groups=mesh['seq'=16,'head'=2] {'seq'}, use_global_device_ids=true, to_apply=%region_19.20 | all-reduce | flops 1120 | bytes 8960 | tf_op jit(solution)/shard_map/psum | solution.py:167
  226.4 48.4 %all-reduce.6.cloned.1.call-done = (f32[8,128,128]{1,2,0:T(8,128)}, f32[8,128,128]{2,1,0:T(8,128)}) async-done(((f32[8,128,128]{1,2,0:T(8,128)}, f32[8,128,128]{2,1,0:T(8,128)}), (f32[8,128,128]{1,2,0:T(8,128)}, f32[8,128,128]{2,1,0:T(8,128)})) %all-reduce.6.cloned.1.call-update) | async-done | bytes 1048592 | tf_op jit(solution)/shard_map/psum | solution.py:167
  274.8 2.0 copy.139
  276.9 1.9 copy.186
  (147 shorter events, 15.8 us)
Async XLA Ops:
  7.2 79.6 %copy-start = (f32[8,128,128]{2,1,0:T(8,128)S(1)}, f32[8,128,128]{2,1,0:T(8,128)}, u32[]{:S(2)}) copy-start(f32[8,128,128]{2,1,0:T(8,128)} %param.15) | copy-start | bytes 1572868
  7.2 86.8 %copy-start.8 = (bf16[128,1024]{1,0:T(8,128)(2,1)S(1)}, bf16[128,1024]{1,0:T(8,128)(2,1)}, u32[]{:S(2)}) copy-start(bf16[128,1024]{1,0:T(8,128)(2,1)} %param.10) | copy-start | bytes 786436
  7.2 86.8 %all-gather.6.cloned.1.call-start = ((), (), s32[]{:S(2)}) async-start(), calls=%async_computation | async-start | bytes 1114112 | tf_op jit(solution)/shard_map/all_gather | solution.py:14
  8.7 117.8 %all-gather.8.cloned.1.call-start = ((), (), s32[]{:S(2)}) async-start(), calls=%async_computation.1 | async-start | bytes 8912896 | tf_op jit(solution)/shard_map/all_gather | solution.py:61
  51.1 223.8 %all-reduce.6.cloned.1.call-start = ((), (), s32[]{:S(2)}) async-start(), calls=%async_computation.2 | async-start | bytes 2097152 | tf_op jit(solution)/shard_map/psum | solution.py:167
  84.2 6.3 %copy-start.25 = (f32[8]{0:T(128)}, f32[8]{0:T(128)S(1)}, u32[]{:S(2)}) copy-start(f32[8]{0:T(128)S(1)} %get-tuple-element.131) | copy-start | bytes 100
  84.2 6.3 %copy-start.26 = (f32[8]{0:T(128)}, f32[8]{0:T(128)S(1)}, u32[]{:S(2)}) copy-start(f32[8]{0:T(128)S(1)} %get-tuple-element.132) | copy-start | bytes 100
  84.2 6.3 %copy-start.27 = (f32[8]{0:T(128)}, f32[8]{0:T(128)S(1)}, u32[]{:S(2)}) copy-start(f32[8]{0:T(128)S(1)} %get-tuple-element.133) | copy-start | bytes 100
  84.3 6.3 %copy-start.28 = (f32[8]{0:T(128)}, f32[8]{0:T(128)S(1)}, u32[]{:S(2)}) copy-start(f32[8]{0:T(128)S(1)} %get-tuple-element.134) | copy-start | bytes 100
  84.3 6.3 %copy-start.29 = (f32[8]{0:T(128)}, f32[8]{0:T(128)S(1)}, u32[]{:S(2)}) copy-start(f32[8]{0:T(128)S(1)} %get-tuple-element.135) | copy-start | bytes 100
  84.3 6.3 %copy-start.30 = (f32[8]{0:T(128)}, f32[8]{0:T(128)S(1)}, u32[]{:S(2)}) copy-start(f32[8]{0:T(128)S(1)} %get-tuple-element.136) | copy-start | bytes 100
  84.4 12.1 %copy-start.14 = (f32[128,128]{1,0:T(8,128)}, f32[128,128]{1,0:T(8,128)S(1)}, u32[]{:S(2)}) copy-start(f32[128,128]{1,0:T(8,128)S(1)} %compare_convert_fusion.7) | copy-start | bytes 196612
  84.5 9.2 %copy-start.15 = (f32[128,128]{1,0:T(8,128)}, f32[128,128]{1,0:T(8,128)S(1)}, u32[]{:S(2)}) copy-start(f32[128,128]{1,0:T(8,128)S(1)} %get-tuple-element.165) | copy-start | bytes 196612
  84.5 9.2 %copy-start.16 = (f32[128,128]{1,0:T(8,128)}, f32[128,128]{1,0:T(8,128)S(1)}, u32[]{:S(2)}) copy-start(f32[128,128]{1,0:T(8,128)S(1)} %get-tuple-element.166) | copy-start | bytes 196612
  84.6 9.1 %copy-start.17 = (f32[128,128]{1,0:T(8,128)}, f32[128,128]{1,0:T(8,128)S(1)}, u32[]{:S(2)}) copy-start(f32[128,128]{1,0:T(8,128)S(1)} %get-tuple-element.163) | copy-start | bytes 196612
  84.6 9.1 %copy-start.18 = (f32[128,128]{1,0:T(8,128)}, f32[128,128]{1,0:T(8,128)S(1)}, u32[]{:S(2)}) copy-start(f32[128,128]{1,0:T(8,128)S(1)} %get-tuple-element.164) | copy-start | bytes 196612
  84.7 9.0 %copy-start.19 = (f32[128,128]{1,0:T(8,128)}, f32[128,128]{1,0:T(8,128)S(1)}, u32[]{:S(2)}) copy-start(f32[128,128]{1,0:T(8,128)S(1)} %get-tuple-element.161) | copy-start | bytes 196612
  84.7 9.0 %copy-start.20 = (f32[128,128]{1,0:T(8,128)}, f32[128,128]{1,0:T(8,128)S(1)}, u32[]{:S(2)}) copy-start(f32[128,128]{1,0:T(8,128)S(1)} %get-tuple-element.162) | copy-start | bytes 196612
  93.9 7.5 %copy-start.9 = (pred[128,2048]{0,1:T(8,128)(4,1)}, pred[128,2048]{0,1:T(8,128)(4,1)S(1)}, u32[]{:S(2)}) copy-start(pred[128,2048]{0,1:T(8,128)(4,1)S(1)} %iota_compare_fusion) | copy-start | bytes 786436
  126.5 19.1 %copy-start.11 = (f32[8,128,128]{2,1,0:T(8,128)S(1)}, f32[8,128,128]{2,1,0:T(8,128)}, u32[]{:S(2)}) copy-start(f32[8,128,128]{2,1,0:T(8,128)} %fusion.25) | copy-start | bytes 1572868
  126.5 26.5 %copy-start.22 = (f32[1024]{0:T(1024)S(1)}, f32[1024]{0:T(1024)}, u32[]{:S(2)}) copy-start(f32[1024]{0:T(1024)} %param.17) | copy-start | bytes 12292
  153.1 15.0 %copy-start.13 = (bf16[128,128]{1,0:T(8,128)(2,1)S(1)}, bf16[128,128]{1,0:T(8,128)(2,1)}, u32[]{:S(2)}) copy-start(bf16[128,128]{1,0:T(8,128)(2,1)} %param.12) | copy-start | bytes 98308
  160.2 17.9 %copy-start.12 = (bf16[128,128]{1,0:T(8,128)(2,1)S(1)}, bf16[128,128]{1,0:T(8,128)(2,1)}, u32[]{:S(2)}) copy-start(bf16[128,128]{1,0:T(8,128)(2,1)} %param.11) | copy-start | bytes 98308
  165.9 11.4 %copy-start.5 = (f32[8,128,128]{2,1,0:T(8,128)S(1)}, f32[8,128,128]{2,1,0:T(8,128)}, u32[]{:S(2)}) copy-start(f32[8,128,128]{2,1,0:T(8,128)} %copy-done.4) | copy-start | bytes 1572868
  165.9 13.9 %copy-start.3 = (f32[8,1,128,128]{3,1,2,0:T(1,128)S(1)}, f32[8,1,128,128]{3,1,2,0:T(1,128)}, u32[]{:S(2)}) copy-start(f32[8,1,128,128]{3,1,2,0:T(1,128)} %copy-done.2) | copy-start | bytes 1572868
  170.8 14.5 %copy-start.38 = (f32[8]{0:T(128)S(1)}, f32[8]{0:T(128)}, u32[]{:S(2)}) copy-start(f32[8]{0:T(128)} %get-tuple-element.122) | copy-start | bytes 100
  170.8 14.5 %copy-start.37 = (f32[8]{0:T(128)S(1)}, f32[8]{0:T(128)}, u32[]{:S(2)}) copy-start(f32[8]{0:T(128)} %get-tuple-element.121) | copy-start | bytes 100
  170.8 14.6 %copy-start.36 = (f32[8]{0:T(128)S(1)}, f32[8]{0:T(128)}, u32[]{:S(2)}) copy-start(f32[8]{0:T(128)} %get-tuple-element.123) | copy-start | bytes 100
  170.8 14.7 %copy-start.35 = (f32[8]{0:T(128)S(1)}, f32[8]{0:T(128)}, u32[]{:S(2)}) copy-start(f32[8]{0:T(128)} %get-tuple-element.124) | copy-start | bytes 100
  170.8 14.8 %copy-start.34 = (f32[8]{0:T(128)S(1)}, f32[8]{0:T(128)}, u32[]{:S(2)}) copy-start(f32[8]{0:T(128)} %get-tuple-element.125) | copy-start | bytes 100
  170.8 14.9 %copy-start.33 = (f32[8]{0:T(128)S(1)}, f32[8]{0:T(128)}, u32[]{:S(2)}) copy-start(f32[8]{0:T(128)} %get-tuple-element.126) | copy-start | bytes 100
  170.8 14.9 %copy-start.32 = (f32[8]{0:T(128)S(1)}, f32[8]{0:T(128)}, u32[]{:S(2)}) copy-start(f32[8]{0:T(128)} %get-tuple-element.127) | copy-start | bytes 100
  (11 other events, 29.7 us)
Sparse Core Ops, SparseCore 0:
  10.2 40.6 all-gather.5
  53.0 73.4 all-gather.7
  182.0 92.7 all-reduce.5
